TPU v7x, 32 devices: a whole 2x2x4 slice. The times are simulated.
32 devices in a mesh: plane: 4 (over y, x), tile: 8 (over z, core).
Axes of the slice: x: 2, y: 2, z: 4, core: 2. Of those that a mesh axis runs over, the one named last changes fastest.
Arguments:
- visibility: float32 [2, 65536], P(None, ('plane', 'tile')), may hold values from -6 to 6
- target: int32 [65536, 1], P(('plane', 'tile')), may hold values from 0 to 31; in each aligned block of 2048 rows (0 to 2047, 2048 to 4095, ...) at most 128 rows name the same one
- offset: int32 [65536], P(('plane', 'tile')), may hold values from 0 to 2097151
- taps: float32 [8], replicated, may hold values from 0.1 to 1
- w_plane: float32 [4], P('plane'), may hold values from -300 to 300
Outputs:
- dirty_image: float32 [4096, 4096], P('plane', 'tile')
Inputs may be any that keep to these rules, and one draw needn't show every extreme that they name: `target`: among the rows of one device no value occurs more than 128 times, and some value occurs exactly 128 times.
All inputs are finite; a program needn't handle non-finite values.
Results may differ from a plain program's by a relative error of at most 0.0042.
Values sent between devices are 32-bit elements; how exact they have to be, the bound alone decides.
A program may use at most 128 MiB of HBM per device.

v0:
```python
import math
import jax
import jax.numpy as jnp
from jax import lax
from jax.sharding import PartitionSpec as P

G = 4096
HIGHEST = lax.Precision.HIGHEST


def shifted(x, axis, by):
    length = lax.axis_size(axis)
    return lax.ppermute(x, axis, [(i, (i + by) % length) for i in range(length)])


def direction(index, length):
    return ((index + length // 2) % length - length // 2).astype(jnp.float32) * (0.5 / length)


def angle_table(first, second, length):
    product = (
        jnp.arange(first, dtype=jnp.int32)[:, None]
        * jnp.arange(second, dtype=jnp.int32)[None, :]
        % length
    )
    angles = product.astype(jnp.float32) * (2.0 * math.pi / length)
    return (jnp.cos(angles), jnp.sin(angles))


def split_length(length):
    inner_len = math.gcd(length, 128)
    return (length // inner_len, inner_len)


def transform_last(real_part, imag_part):
    length = real_part.shape[-1]
    outer_len, inner_len = split_length(length)
    real_grid = real_part.reshape(-1, outer_len, inner_len)
    imag_grid = imag_part.reshape(-1, outer_len, inner_len)
    cos_one, sin_one = angle_table(outer_len, outer_len, outer_len)
    first_re = jnp.einsum("rab,ak->rkb", real_grid, cos_one, precision=HIGHEST) - jnp.einsum(
        "rab,ak->rkb", imag_grid, sin_one, precision=HIGHEST
    )
    first_im = jnp.einsum("rab,ak->rkb", real_grid, sin_one, precision=HIGHEST) + jnp.einsum(
        "rab,ak->rkb", imag_grid, cos_one, precision=HIGHEST
    )
    cos_tw, sin_tw = angle_table(outer_len, inner_len, length)
    twist_re = first_re * cos_tw - first_im * sin_tw
    twist_im = first_re * sin_tw + first_im * cos_tw
    cos_two, sin_two = angle_table(inner_len, inner_len, inner_len)
    out_re = jnp.einsum("rkb,bq->rqk", twist_re, cos_two, precision=HIGHEST) - jnp.einsum(
        "rkb,bq->rqk", twist_im, sin_two, precision=HIGHEST
    )
    out_im = jnp.einsum("rkb,bq->rqk", twist_re, sin_two, precision=HIGHEST) + jnp.einsum(
        "rkb,bq->rqk", twist_im, cos_two, precision=HIGHEST
    )
    return (out_re.reshape(-1, length), out_im.reshape(-1, length))


def transform_first(real_part, imag_part):
    length = real_part.shape[0]
    outer_len, inner_len = split_length(length)
    real_grid = real_part.reshape(outer_len, inner_len, -1)
    imag_grid = imag_part.reshape(outer_len, inner_len, -1)
    cos_one, sin_one = angle_table(outer_len, outer_len, outer_len)
    first_re = jnp.einsum("abc,ak->kbc", real_grid, cos_one, precision=HIGHEST) - jnp.einsum(
        "abc,ak->kbc", imag_grid, sin_one, precision=HIGHEST
    )
    first_im = jnp.einsum("abc,ak->kbc", real_grid, sin_one, precision=HIGHEST) + jnp.einsum(
        "abc,ak->kbc", imag_grid, cos_one, precision=HIGHEST
    )
    cos_tw, sin_tw = angle_table(outer_len, inner_len, length)
    twist_re = first_re * cos_tw[:, :, None] - first_im * sin_tw[:, :, None]
    twist_im = first_re * sin_tw[:, :, None] + first_im * cos_tw[:, :, None]
    cos_two, sin_two = angle_table(inner_len, inner_len, inner_len)
    out_re = jnp.einsum("kbc,bq->qkc", twist_re, cos_two, precision=HIGHEST) - jnp.einsum(
        "kbc,bq->qkc", twist_im, sin_two, precision=HIGHEST
    )
    out_im = jnp.einsum("kbc,bq->qkc", twist_re, sin_two, precision=HIGHEST) + jnp.einsum(
        "kbc,bq->qkc", twist_im, cos_two, precision=HIGHEST
    )
    return (out_re.reshape(length, -1), out_im.reshape(length, -1))


def grid_block(received, taps, start, block_len, band_rows, totals):
    piece = lax.dynamic_slice_in_dim(received, start, block_len, 1)
    encoded = jnp.maximum(piece[2].astype(jnp.int32) - 1, 0)
    band_row = encoded // G
    column = encoded % G
    kernel_len = taps.shape[0]
    taps_low = taps.astype(jnp.bfloat16)
    weight_re = (taps[None, :] * piece[0][:, None]).astype(jnp.bfloat16)
    weight_im = (taps[None, :] * piece[1][:, None]).astype(jnp.bfloat16)
    rel_row = jnp.arange(band_rows, dtype=jnp.int32)[None, :] - band_row[:, None]
    rel_col = (jnp.arange(G, dtype=jnp.int32)[None, :] - column[:, None]) % G
    row_re = jnp.zeros((block_len, band_rows), jnp.bfloat16)
    row_im = jnp.zeros((block_len, band_rows), jnp.bfloat16)
    col_table = jnp.zeros((block_len, G), jnp.bfloat16)
    for tap_index in range(kernel_len):
        row_re = jnp.where(rel_row == tap_index, weight_re[:, tap_index : tap_index + 1], row_re)
        row_im = jnp.where(rel_row == tap_index, weight_im[:, tap_index : tap_index + 1], row_im)
        col_table = jnp.where(rel_col == tap_index, taps_low[tap_index], col_table)
    row_table = jnp.concatenate([row_re, row_im], axis=1)
    return totals + lax.dot_general(
        row_table, col_table, (((0,), (0,)), ((), ())), preferred_element_type=jnp.float32
    )


def local(visibility, target, offset, taps, w_plane):
    tiles = lax.axis_size("tile")
    planes = lax.axis_size("plane")
    devices = tiles * planes
    vis_dev = visibility.shape[1]
    capacity = 2 * vis_dev // devices
    slot_total = devices * capacity
    band = G // tiles
    columns = G // tiles
    kernel_len = taps.shape[0]
    band_rows = band + kernel_len - 1
    destination = target[:, 0]
    onehot = (destination[:, None] == jnp.arange(devices, dtype=jnp.int32)[None, :]).astype(
        jnp.int32
    )
    rank = jnp.sum(jnp.cumsum(onehot, axis=0) * onehot, axis=1) - 1
    slot = destination * capacity + rank
    payload = jnp.stack([visibility[0], visibility[1], offset.astype(jnp.float32) + 1.0])
    outgoing = jnp.zeros((3, slot_total), jnp.float32).at[:, slot].set(payload)
    received = lax.all_to_all(outgoing, ("plane", "tile"), split_axis=1, concat_axis=1, tiled=True)
    block_len = min(512, slot_total)
    empty = jnp.zeros((2 * band_rows, G), jnp.float32)

    def grid_step(index, totals):
        return grid_block(received, taps, index * block_len, block_len, band_rows, totals)

    gridded = lax.fori_loop(0, slot_total // block_len, grid_step, empty)
    gridded = gridded.reshape(2, band_rows, G)
    incoming = shifted(gridded[:, band:], "tile", 1)
    grid_band = gridded[:, :band].at[:, : kernel_len - 1].add(incoming)
    col_re, col_im = transform_last(grid_band[0], grid_band[1])
    stacked = jnp.stack([col_re, col_im]).reshape(2, band, tiles, columns)
    exchanged = lax.all_to_all(stacked, "tile", split_axis=2, concat_axis=1, tiled=True)
    item_count = exchanged.shape[3]
    rows_re, rows_im = transform_first(
        exchanged[0].reshape(G, item_count), exchanged[1].reshape(G, item_count)
    )
    image_parts = jnp.stack([rows_re, rows_im]).reshape(2, G, 1, item_count).reshape(2, G, columns)
    line_pos = jnp.arange(G, dtype=jnp.int32)
    column_pos = lax.axis_index("tile") * columns + jnp.arange(columns, dtype=jnp.int32)
    cos_row = direction(line_pos, G)
    cos_col = direction(column_pos, G)
    n_minus = (
        jnp.sqrt(1.0 - cos_row[:, None] * cos_row[:, None] - cos_col[None, :] * cos_col[None, :])
        - 1.0
    )
    phase = 2.0 * math.pi * w_plane[0] * n_minus
    screened = jnp.cos(phase) * image_parts[0] - jnp.sin(phase) * image_parts[1]
    summed = lax.psum_scatter(screened, "plane", scatter_dimension=0, tiled=True)
    return summed * (1.0 / math.sqrt(vis_dev * devices))


def solution(mesh):
    return jax.shard_map(
        local,
        mesh=mesh,
        in_specs=(
            P(None, ("plane", "tile")),
            P(("plane", "tile"), None),
            P(("plane", "tile")),
            P(),
            P("plane"),
        ),
        out_specs=P("plane", "tile"),
        check_vma=False,
    )
```

profile of v0, /device:TPU:0, one launch (start us, length us, event | category | flops | bytes accessed | tf_op | source)
XLA Modules:
  0.0 1112.9 jit_solution(1792978015275601666)
XLA Ops:
  7.3 9.1 reduce-window.6
  20.4 6.1 scatter_custom_fusion
  27.7 7.3 all-to-all-start
  35.7 6.7 all-to-all-done
  42.5 216.9 %while.18 = (s32[]{:T(128)}, f32[1038,4096]{1,0:T(8,128)}, f32[3,4096]{1,0:T(4,128)S(1)}, f32[8]{0:T(128)}, bf16[8]{0:T(256)(128)(2,1)S(1)}, /*index=5*/s32[]{:T...) while((s32[]{:T(128)}, f32[1038,4096]{1,0:T(8,128)}, f32[3,4096]{1,0:T(4,128)S(1)}, ...), condition=%wide.region_5.6_spmd.clone, body=%wide.region_4.5_spmd.clone.sunk | while | flops 4429704192 | bytes 36240668 | solution.py:135
  46.1 20.6 %select_add_fusion.2 = f32[1038,4096]{1,0:T(8,128)} fusion(f32[1038,4096]{1,0:T(8,128)} %get-tuple-element.356, pred[]{:T(512)S(6)} %compare.38, s32[512]{0:T(512)S(1)} %get-tuple-element.312, bf16[]{:T(256)} %bitcast.127, bf16[]{:T(256)} %bitcast.128, bf16[]{:T(256)} %bitcast.129, bf16[]{:T(256)} %bitcast.130, bf16[]{:T(256)} %bitcast.131, ...), kind=kOutput, calls=%fused_computation.1.clone.1 | convolution fusion | flops 4423036928 | bytes 35078160 | tf_op jit(solution)/shard_map/while/body/eval_jaxpr/dot_general | solution.py:104
  67.7 1.9 fusion.257
  70.2 23.9 %select_add_fusion.2 = f32[1038,4096]{1,0:T(8,128)} fusion(f32[1038,4096]{1,0:T(8,128)} %get-tuple-element.356, pred[]{:T(512)S(6)} %compare.38, s32[512]{0:T(512)S(1)} %get-tuple-element.312, bf16[]{:T(256)} %bitcast.127, bf16[]{:T(256)} %bitcast.128, bf16[]{:T(256)} %bitcast.129, bf16[]{:T(256)} %bitcast.130, bf16[]{:T(256)} %bitcast.131, ...), kind=kOutput, calls=%fused_computation.1.clone.1 | convolution fusion | flops 4423036928 | bytes 35078160 | tf_op jit(solution)/shard_map/while/body/eval_jaxpr/dot_general | solution.py:104
  95.2 1.9 fusion.257
  97.7 23.9 %select_add_fusion.2 = f32[1038,4096]{1,0:T(8,128)} fusion(f32[1038,4096]{1,0:T(8,128)} %get-tuple-element.356, pred[]{:T(512)S(6)} %compare.38, s32[512]{0:T(512)S(1)} %get-tuple-element.312, bf16[]{:T(256)} %bitcast.127, bf16[]{:T(256)} %bitcast.128, bf16[]{:T(256)} %bitcast.129, bf16[]{:T(256)} %bitcast.130, bf16[]{:T(256)} %bitcast.131, ...), kind=kOutput, calls=%fused_computation.1.clone.1 | convolution fusion | flops 4423036928 | bytes 35078160 | tf_op jit(solution)/shard_map/while/body/eval_jaxpr/dot_general | solution.py:104
  125.3 23.9 %select_add_fusion.2 = f32[1038,4096]{1,0:T(8,128)} fusion(f32[1038,4096]{1,0:T(8,128)} %get-tuple-element.356, pred[]{:T(512)S(6)} %compare.38, s32[512]{0:T(512)S(1)} %get-tuple-element.312, bf16[]{:T(256)} %bitcast.127, bf16[]{:T(256)} %bitcast.128, bf16[]{:T(256)} %bitcast.129, bf16[]{:T(256)} %bitcast.130, bf16[]{:T(256)} %bitcast.131, ...), kind=kOutput, calls=%fused_computation.1.clone.1 | convolution fusion | flops 4423036928 | bytes 35078160 | tf_op jit(solution)/shard_map/while/body/eval_jaxpr/dot_general | solution.py:104
  152.8 23.9 %select_add_fusion.2 = f32[1038,4096]{1,0:T(8,128)} fusion(f32[1038,4096]{1,0:T(8,128)} %get-tuple-element.356, pred[]{:T(512)S(6)} %compare.38, s32[512]{0:T(512)S(1)} %get-tuple-element.312, bf16[]{:T(256)} %bitcast.127, bf16[]{:T(256)} %bitcast.128, bf16[]{:T(256)} %bitcast.129, bf16[]{:T(256)} %bitcast.130, bf16[]{:T(256)} %bitcast.131, ...), kind=kOutput, calls=%fused_computation.1.clone.1 | convolution fusion | flops 4423036928 | bytes 35078160 | tf_op jit(solution)/shard_map/while/body/eval_jaxpr/dot_general | solution.py:104
  180.4 23.9 %select_add_fusion.2 = f32[1038,4096]{1,0:T(8,128)} fusion(f32[1038,4096]{1,0:T(8,128)} %get-tuple-element.356, pred[]{:T(512)S(6)} %compare.38, s32[512]{0:T(512)S(1)} %get-tuple-element.312, bf16[]{:T(256)} %bitcast.127, bf16[]{:T(256)} %bitcast.128, bf16[]{:T(256)} %bitcast.129, bf16[]{:T(256)} %bitcast.130, bf16[]{:T(256)} %bitcast.131, ...), kind=kOutput, calls=%fused_computation.1.clone.1 | convolution fusion | flops 4423036928 | bytes 35078160 | tf_op jit(solution)/shard_map/while/body/eval_jaxpr/dot_general | solution.py:104
  207.9 23.9 %select_add_fusion.2 = f32[1038,4096]{1,0:T(8,128)} fusion(f32[1038,4096]{1,0:T(8,128)} %get-tuple-element.356, pred[]{:T(512)S(6)} %compare.38, s32[512]{0:T(512)S(1)} %get-tuple-element.312, bf16[]{:T(256)} %bitcast.127, bf16[]{:T(256)} %bitcast.128, bf16[]{:T(256)} %bitcast.129, bf16[]{:T(256)} %bitcast.130, bf16[]{:T(256)} %bitcast.131, ...), kind=kOutput, calls=%fused_computation.1.clone.1 | convolution fusion | flops 4423036928 | bytes 35078160 | tf_op jit(solution)/shard_map/while/body/eval_jaxpr/dot_general | solution.py:104
  235.4 23.9 %select_add_fusion.2 = f32[1038,4096]{1,0:T(8,128)} fusion(f32[1038,4096]{1,0:T(8,128)} %get-tuple-element.356, pred[]{:T(512)S(6)} %compare.38, s32[512]{0:T(512)S(1)} %get-tuple-element.312, bf16[]{:T(256)} %bitcast.127, bf16[]{:T(256)} %bitcast.128, bf16[]{:T(256)} %bitcast.129, bf16[]{:T(256)} %bitcast.130, bf16[]{:T(256)} %bitcast.131, ...), kind=kOutput, calls=%fused_computation.1.clone.1 | convolution fusion | flops 4423036928 | bytes 35078160 | tf_op jit(solution)/shard_map/while/body/eval_jaxpr/dot_general | solution.py:104
  259.4 13.3 %reshape.237 = f32[2,519,4096]{2,1,0:T(8,128)} reshape(f32[1038,4096]{1,0:T(8,128)} %get-tuple-element.158) | data formatting | bytes 34013184 | tf_op jit(solution)/shard_map/reshape | solution.py:136
  274.1 11.5 %slice.405 = f32[2,512,4096]{2,1,0:T(8,128)} slice(f32[2,519,4096]{2,1,0:T(8,128)} %reshape.237), slice={[0:2], [0:512], [0:4096]} | slice | bytes 33554432 | tf_op jit(solution)/shard_map/slice | solution.py:138
  288.4 10.1 slice_bitcast_fusion
  298.5 5.2 copy.69
  303.7 9.5 fusion.145
  313.2 9.7 fusion.149
  324.8 9.5 fusion.143
  334.3 19.1 %subtract_bitcast_fusion.1 = (f32[512,32,128]{2,1,0:T(8,128)}, f32[512,32,128]{2,1,0:T(8,128)}) fusion(f32[32,128]{1,0:T(8,128)S(1)} %get-tuple-element.239, f32[32,128]{1,0:T(8,128)S(1)} %get-tuple-element.240, f32[32,512,128]{2,0,1:T(8,128)} %fusion.143, f32[32,512,128]{2,0,1:T(8,128)} %fusion.149, f32[32,512,128]{2,0,1:T(8,128)} %fusion.145, ...), kind=kOutput, calls=%fused_computation.116 | convolution fusion | flops 822097920 | bytes 50364416 | tf_op jit(solution)/shard_map/rab,ak->rkb/dot_general | solution.py:41
  353.4 21.6 %fusion.84 = f32[128,512,32]{1,0,2:T(8,128)} fusion(f32[512,32,128]{2,1,0:T(8,128)} %get-tuple-element.234), kind=kOutput, calls=%fused_computation.135 | convolution fusion | flops 3221454848 | bytes 16777216 | tf_op jit(solution)/shard_map/rkb,bq->rqk/dot_general | solution.py:51
  375.0 16.1 %fusion.82 = f32[128,512,32]{1,0,2:T(8,128)S(1)} fusion(f32[512,32,128]{2,1,0:T(8,128)S(1)} %copy-done.2), kind=kOutput, calls=%fused_computation.133 | convolution fusion | flops 3221454848 | bytes 16777216 | tf_op jit(solution)/shard_map/rkb,bq->rqk/dot_general | solution.py:54
  391.1 15.9 %subtract_bitcast_fusion = f32[512,128,32]{0,1,2:T(8,128)} fusion(f32[128,512,32]{1,0,2:T(8,128)} %fusion.84, f32[512,32,128]{2,1,0:T(8,128)S(1)} %bitcast.140), kind=kOutput, calls=%fused_computation.114 | convolution fusion | flops 3223552000 | bytes 25165824 | tf_op jit(solution)/shard_map/rkb,bq->rqk/dot_general | solution.py:51
  407.0 11.5 %copy.48 = f32[512,128,32]{0,2,1:T(8,128)} copy(f32[512,128,32]{0,1,2:T(8,128)} %subtract_bitcast_fusion) | data formatting | bytes 16777216 | tf_op jit(solution)/shard_map/sub | solution.py:51
  418.5 13.7 %add_bitcast_fusion = f32[512,128,32]{0,1,2:T(8,128)} fusion(f32[128,512,32]{1,0,2:T(8,128)S(1)} %fusion.82, f32[512,32,128]{2,1,0:T(8,128)S(1)} %bitcast.140), kind=kOutput, calls=%fused_computation.113 | convolution fusion | flops 3223552000 | bytes 25165824 | tf_op jit(solution)/shard_map/rkb,bq->rqk/dot_general | solution.py:54
  432.2 8.4 copy.51
  440.6 1.9 pad_maximum_fusion
  442.6 6.2 copy.52
  448.7 5.8 all-to-all-start.1
  455.4 362.7 %all-to-all-done.1 = f32[2,512,8,512]{1,3,0,2:T(8,128)} async-done(((f32[2,512,8,512]{1,3,0,2:T(8,128)}), f32[2,512,8,512]{1,3,0,2:T(8,128)}, u32[]{:S(2)}, u32[]{:S(2)}) %all-to-all-start.1) | async-done | bytes 16777248 | tf_op jit(solution)/shard_map/all_to_all | solution.py:141
  818.1 17.6 %copy.53 = f32[2,512,8,512]{3,1,2,0:T(8,128)} copy(f32[2,512,8,512]{1,3,0,2:T(8,128)} %all-to-all-done.1) | data formatting | bytes 33554432 | tf_op jit(solution)/shard_map/all_to_all | solution.py:141
  835.7 6.9 fusion.245
  842.6 13.2 %fusion.74 = f32[32,128,512]{2,0,1:T(8,128)} fusion(f32[32,128,512]{2,1,0:T(8,128)S(1)} %bitcast.145), kind=kOutput, calls=%fused_computation.125 | convolution fusion | flops 805320704 | bytes 16777216 | tf_op jit(solution)/shard_map/abc,ak->kbc/dot_general | solution.py:69
  855.8 13.4 %fusion.76 = f32[32,128,512]{2,0,1:T(8,128)} fusion(f32[32,128,512]{2,1,0:T(8,128)S(1)} %bitcast.146), kind=kOutput, calls=%fused_computation.127 | convolution fusion | flops 805320704 | bytes 16777216 | tf_op jit(solution)/shard_map/abc,ak->kbc/dot_general | solution.py:66
  869.3 13.2 %fusion.80 = f32[32,128,512]{2,0,1:T(8,128)} fusion(f32[32,128,512]{2,1,0:T(8,128)S(1)} %bitcast.147), kind=kOutput, calls=%fused_computation.131 | convolution fusion | flops 805320704 | bytes 16777216 | tf_op jit(solution)/shard_map/abc,ak->kbc/dot_general | solution.py:66
  882.4 24.2 %multiply_subtract_fusion = (f32[32,128,512]{2,0,1:T(8,128)}, f32[32,128,512]{2,0,1:T(8,128)}) fusion(f32[32,128]{0,1:T(8,128)S(1)} %copy.59, f32[32,128]{0,1:T(8,128)S(1)} %copy.56, f32[32,128,512]{2,0,1:T(8,128)} %fusion.74, f32[32,128,512]{2,0,1:T(8,128)} %fusion.80, f32[32,128,512]{2,0,1:T(8,128)} %fusion.76, f32[32,128,512]{2,1,0:T(8,128)} %bitcast.148), kind=kOutput, calls=%fused_computation.112 | convolution fusion | flops 822097920 | bytes 50364416 | tf_op jit(solution)/shard_map/abc,ak->kbc/dot_general | solution.py:69
  906.7 17.0 %fusion.68 = f32[128,32,512]{2,0,1:T(8,128)S(1)} fusion(f32[32,128,512]{2,0,1:T(8,128)} %get-tuple-element.232), kind=kOutput, calls=%fused_computation.119 | convolution fusion | flops 3221454848 | bytes 16777216 | tf_op jit(solution)/shard_map/kbc,bq->qkc/dot_general | solution.py:76
  923.7 13.6 %fusion.66 = f32[128,32,512]{2,0,1:T(8,128)} fusion(f32[32,128,512]{2,0,1:T(8,128)S(1)} %copy-done), kind=kOutput, calls=%fused_computation.117 | convolution fusion | flops 3221454848 | bytes 16777216 | tf_op jit(solution)/shard_map/kbc,bq->qkc/dot_general | solution.py:79
  937.3 13.6 %fusion.94 = f32[128,32,512]{2,0,1:T(8,128)} fusion(f32[128,32,512]{2,0,1:T(8,128)S(1)} %fusion.68, f32[32,128,512]{2,0,1:T(8,128)S(1)} %bitcast.138), kind=kOutput, calls=%fused_computation.141 | convolution fusion | flops 3223552000 | bytes 25165824 | tf_op jit(solution)/shard_map/kbc,bq->qkc/dot_general | solution.py:76
  950.9 8.2 copy.62
  959.1 15.6 %fusion.97 = f32[128,32,512]{2,0,1:T(8,128)} fusion(f32[128,32,512]{2,0,1:T(8,128)} %fusion.66, f32[32,128,512]{2,0,1:T(8,128)S(1)} %bitcast.138), kind=kOutput, calls=%fused_computation.142 | convolution fusion | flops 3223552000 | bytes 25165824 | tf_op jit(solution)/shard_map/kbc,bq->qkc/dot_general | solution.py:79
  974.8 8.2 copy.65
  983.0 36.1 %fusion.65 = f32[4096,512]{1,0:T(8,128)} fusion(f32[128,32,512]{2,1,0:T(8,128)S(1)} %copy.65, f32[128,32,512]{2,1,0:T(8,128)S(1)} %copy.62, f32[512]{0:T(512)S(1)} %fusion.178, f32[4096]{0:T(1024)S(1)} %fusion.134, f32[]{:T(128)} %bitcast), kind=kLoop, calls=%fused_computation.109 | loop fusion | flops 12582912 | bytes 25184260 | tf_op jit(solution)/shard_map/sub | solution.py:156
  1019.1 83.6 %reduce-scatter.2.cloned.1.call-done = f32[1024,512]{1,0:T(8,128)} async-done(((f32[4096,512]{1,0:T(8,128)}), f32[1024,512]{1,0:T(8,128)}) %reduce-scatter.2.cloned.1.call-update) | async-done | bytes 2097168 | tf_op jit(solution)/shard_map/reduce_scatter | solution.py:157
  1102.7 3.1 broadcast_multiply_fusion
  (109 shorter events, 37.8 us)
Async XLA Ops:
  27.7 14.7 %all-to-all-start = ((f32[3,32,128]{2,0,1:T(4,128)}), f32[3,32,128]{2,0,1:T(4,128)S(1)}, u32[]{:S(2)}, u32[]{:S(2)}) async-start(f32[3,32,128]{2,0,1:T(4,128)} %copy.45), calls=%async_computation | async-start | bytes 131072 | tf_op jit(solution)/shard_map/all_to_all | solution.py:128
  273.6 12.0 %collective-permute-start = (f32[2,7,4096]{2,1,0:T(8,128)S(1)}, f32[2,7,4096]{2,1,0:T(8,128)S(1)}, u32[]{:S(2)}, u32[]{:S(2)}) collective-permute-start(f32[2,7,4096]{2,1,0:T(8,128)S(1)} %slice.407), channel_id=1, source_target_pairs={{0,1},{1,2},{2,3},{3,4},{4,5},{5,6},{6,7},{7,0},{8,9},{9,10},{10,1... | collective-permute-start | bytes 688136 | tf_op jit(solution)/shard_map/ppermute | solution.py:13
  324.8 9.5 copy-start.1
  353.4 21.6 %copy-start.2 = (f32[512,32,128]{2,1,0:T(8,128)S(1)}, f32[512,32,128]{2,1,0:T(8,128)}, u32[]{:S(2)}) copy-start(f32[512,32,128]{2,1,0:T(8,128)} %get-tuple-element.234) | copy-start | bytes 25165828
  353.4 37.7 %slice-start.2 = ((s8[8388608]{0:T(1024)(128)(4,1)}), s8[4194304]{0:T(1024)(128)(4,1)S(1)}, s32[]{:S(2)}) async-start(s8[8388608]{0:T(1024)(128)(4,1)} %bitcast.139), calls=%async_computation.6 | async-start | bytes 8388608
  375.0 16.1 %slice-start.3 = ((s8[8388608]{0:T(1024)(128)(4,1)}), s8[4194304]{0:T(1024)(128)(4,1)S(1)}, s32[]{:S(2)}) async-start(s8[8388608]{0:T(1024)(128)(4,1)} %bitcast.139), calls=%async_computation.7 | async-start | bytes 8388608
  432.2 8.4 copy-start.4
  448.7 369.4 %all-to-all-start.1 = ((f32[2,512,8,512]{1,3,0,2:T(8,128)}), f32[2,512,8,512]{1,3,0,2:T(8,128)}, u32[]{:S(2)}, u32[]{:S(2)}) async-start(f32[2,512,8,512]{1,3,0,2:T(8,128)} %copy.52), calls=%async_computation.1 | async-start | bytes 33554432 | tf_op jit(solution)/shard_map/all_to_all | solution.py:141
  454.5 648.2 %reduce-scatter.2.cloned.1.call-start = ((), (), s32[]{:S(2)}) async-start(), calls=%async_computation.3 | async-start | bytes 10485760 | tf_op jit(solution)/shard_map/reduce_scatter | solution.py:157
  842.6 26.7 %copy-start.3 = (f32[1,8,512,1,512]{4,2,1,3,0:T(8,128)}, f32[1,8,512,1,512]{4,2,1,3,0:T(8,128)S(1)}, u32[]{:S(2)}) copy-start(f32[1,8,512,1,512]{4,2,1,3,0:T(8,128)S(1)} %get-tuple-element.236) | copy-start | bytes 25165828
  906.7 17.0 %copy-start = (f32[32,128,512]{2,0,1:T(8,128)S(1)}, f32[32,128,512]{2,0,1:T(8,128)}, u32[]{:S(2)}) copy-start(f32[32,128,512]{2,0,1:T(8,128)} %get-tuple-element.232) | copy-start | bytes 25165828
  906.7 30.6 %slice-start = ((s8[8388608]{0:T(1024)(128)(4,1)}), s8[4194304]{0:T(1024)(128)(4,1)S(1)}, s32[]{:S(2)}) async-start(s8[8388608]{0:T(1024)(128)(4,1)} %bitcast.137), calls=%async_computation.4 | async-start | bytes 8388608
  923.7 13.6 %slice-start.1 = ((s8[8388608]{0:T(1024)(128)(4,1)}), s8[4194304]{0:T(1024)(128)(4,1)S(1)}, s32[]{:S(2)}) async-start(s8[8388608]{0:T(1024)(128)(4,1)} %bitcast.137), calls=%async_computation.5 | async-start | bytes 8388608
Sparse Core Ops, SparseCore 0:
  1019.2 83.4 reduce-scatter.1
where the time goes:
time: 1120 us; the launch traced here: 1110 us
  waiting for transfers between devices  453 us (40%)
  matrix products  427 us (38%)
  local copies, waits for them, and re-layouts  127 us (11%)
  other arithmetic  77.7 us (7%)
  between operations  14.6 us (1%)
  starting transfers between devices  13.5 us (1%)
    all_to_all x1, waiting for transfers between devices, local(): lax.all_to_all(stacked, 'tile', split_axis=2, concat_axis=1, tiled=True)  363 us
    dot_general x8, matrix products, grid_block(): lax.dot_general(row_table, col_table, (((0,), (0,)), ((), ())), preferred...  188 us
    reduce_scatter x1, waiting for transfers between devices, local(): lax.psum_scatter(screened, 'plane', scatter_dimension=0, tiled=True)  83.6 us
    sub x1, other arithmetic, local(): screened = jnp.cos(phase) * image_parts[0] - jnp.sin(phase) * image_parts[1]  36.1 us
    dot_general x1, matrix products, transform_first(): jnp.einsum('abc,ak->kbc', real_grid, sin_one, precision=HIGHEST)  24.2 us
  transfers between devices with their start and end apart: 4, of which 3 were waited for; matrix products, arithmetic and copies ran while one was open for 1% of the time, Pallas kernels for 0%

commit v1 on v0

--- a/solution.py
+++ b/solution.py
@@ -6,6 +6,18 @@
 
 G = 4096
 HIGHEST = lax.Precision.HIGHEST
+
+
+def register_the_lots_all(q_in, on_dim, row_data):
+    v1 = q_in.shape
+    r1 = q_in.reshape(*v1[:on_dim], row_data, v1[on_dim] // row_data, *v1[on_dim + 1 :])
+    return jnp.moveaxis(r1, on_dim, 0)
+
+
+def press_lanes(point, d_out):
+    t_next = list(point.shape[1:])
+    t_next[d_out] *= point.shape[0]
+    return jnp.moveaxis(point, 0, d_out).reshape(t_next)
 
 
 def shifted(x, axis, by):
@@ -138,7 +150,18 @@
     grid_band = gridded[:, :band].at[:, : kernel_len - 1].add(incoming)
     col_re, col_im = transform_last(grid_band[0], grid_band[1])
     stacked = jnp.stack([col_re, col_im]).reshape(2, band, tiles, columns)
-    exchanged = lax.all_to_all(stacked, "tile", split_axis=2, concat_axis=1, tiled=True)
+    y1 = jax.lax.axis_index("tile")
+    n_now = jax.lax.axis_size("tile")
+    e_next, w2 = (n_now, y1)
+    then = register_the_lots_all(stacked, 2, e_next)
+    chunks = [then[w2]]
+    for idx in range(1, e_next):
+        s_next = then[w2 ^ idx]
+        piece_next = jax.lax.ppermute(s_next, "tile", [(u, u ^ idx) for u in range(e_next)])
+        chunks.append(piece_next)
+    state_next = jnp.stack(chunks)
+    then = state_next[w2 ^ jnp.arange(e_next)]
+    exchanged = press_lanes(then, 1)
     item_count = exchanged.shape[3]
     rows_re, rows_im = transform_first(
         exchanged[0].reshape(G, item_count), exchanged[1].reshape(G, item_count)

time: 1120 us -> 1120 us (level)
  waiting for transfers between devices: 453 us -> 411 us
  local copies, waits for them, and re-layouts: 127 us -> 160 us
    all_to_all x1 -> x0, waiting for transfers between devices: 363 us -> none  [local(): lax.all_to_all(stacked, 'tile', split_axis=2, concat_axis=1, tiled=True)]
    ppermute x0 -> x7, waiting for transfers between devices: none -> 236 us  [local(): jax.lax.ppermute(s_next, 'tile', [(u, u ^ idx) for u in range(e_next)])]
    reduce_scatter x1, waiting for transfers between devices: 83.6 us -> 169 us  [local(): lax.psum_scatter(screened, 'plane', scatter_dimension=0, tiled=True)]
    unnamed x21 -> x30, local copies, waits for them, and re-layouts: 17.1 us -> 40.1 us
    all_to_all x1 -> x0, local copies, waits for them, and re-layouts: 17.6 us -> none  [local(): lax.all_to_all(stacked, 'tile', split_axis=2, concat_axis=1, tiled=True)]
    another operation x3 -> x11, local copies, waits for them, and re-layouts: 6.54 us -> 24.1 us  [the longest x1 6.18 us: local(): stacked = jnp.stack([col_re, col_im]).reshape(2, band, tiles, columns)]
    gather x0 -> x1, local copies, waits for them, and re-layouts: none -> 13.9 us  [local(): then = state_next[w2 ^ jnp.arange(e_next)]]
  transfers between devices with their start and end apart: 4 -> 10, of which waited for: 3 -> 5; matrix products, arithmetic and copies ran while one was open for 1% -> 5% of each run, Pallas kernels for 0% -> 0%
where the time goes in v1:
time: 1120 us; the launch traced here: 1110 us
  matrix products  424 us (38%)
  waiting for transfers between devices  411 us (37%)
  local copies, waits for them, and re-layouts  160 us (14%)
  other arithmetic  85.5 us (8%)
  starting transfers between devices  15.9 us (1%)
  between operations  14.8 us (1%)
    ppermute x7, waiting for transfers between devices, local(): jax.lax.ppermute(s_next, 'tile', [(u, u ^ idx) for u in range(e_next)])  236 us
    dot_general x8, matrix products, grid_block(): lax.dot_general(row_table, col_table, (((0,), (0,)), ((), ())), preferred...  188 us
    reduce_scatter x1, waiting for transfers between devices, local(): lax.psum_scatter(screened, 'plane', scatter_dimension=0, tiled=True)  169 us
    unnamed x30, local copies, waits for them, and re-layouts  40.1 us
    sub x1, other arithmetic, local(): screened = jnp.cos(phase) * image_parts[0] - jnp.sin(phase) * image_parts[1]  36.1 us
    dot_general x1, matrix products, transform_first(): jnp.einsum('abc,ak->kbc', real_grid, sin_one, precision=HIGHEST)  24.5 us
    another operation x10, local copies, waits for them, and re-layouts  22.6 us
  transfers between devices with their start and end apart: 10, of which 5 were waited for; matrix products, arithmetic and copies ran while one was open for 5% of the time, Pallas kernels for 0%

profile of v1, /device:TPU:0, one launch (start us, length us, event | category | flops | bytes accessed | tf_op | source)
XLA Modules:
  0.0 1112.5 jit_solution(12979587282691348988)
XLA Ops:
  7.3 9.1 reduce-window.6
  20.4 6.1 scatter_custom_fusion
  27.7 7.3 all-to-all-start
  35.8 6.7 all-to-all-done
  42.5 216.9 %while.18 = (s32[]{:T(128)}, f32[1038,4096]{1,0:T(8,128)}, f32[3,4096]{1,0:T(4,128)S(1)}, f32[8]{0:T(128)}, bf16[8]{0:T(256)(128)(2,1)S(1)}, /*index=5*/s32[]{:T...) while((s32[]{:T(128)}, f32[1038,4096]{1,0:T(8,128)}, f32[3,4096]{1,0:T(4,128)S(1)}, ...), condition=%wide.region_5.6_spmd.clone, body=%wide.region_4.5_spmd.clone.sunk | while | flops 4429704192 | bytes 36240668 | solution.py:147
  46.1 20.6 %select_add_fusion.2 = f32[1038,4096]{1,0:T(8,128)} fusion(f32[1038,4096]{1,0:T(8,128)} %get-tuple-element.364, pred[]{:T(512)S(6)} %compare.38, s32[512]{0:T(512)S(1)} %get-tuple-element.320, bf16[]{:T(256)} %bitcast.153, bf16[]{:T(256)} %bitcast.154, bf16[]{:T(256)} %bitcast.155, bf16[]{:T(256)} %bitcast.156, bf16[]{:T(256)} %bitcast.157, ...), kind=kOutput, calls=%fused_computation.2.clone.1 | convolution fusion | flops 4423036928 | bytes 35078160 | tf_op jit(solution)/shard_map/while/body/eval_jaxpr/dot_general | solution.py:116
  70.2 23.9 %select_add_fusion.2 = f32[1038,4096]{1,0:T(8,128)} fusion(f32[1038,4096]{1,0:T(8,128)} %get-tuple-element.364, pred[]{:T(512)S(6)} %compare.38, s32[512]{0:T(512)S(1)} %get-tuple-element.320, bf16[]{:T(256)} %bitcast.153, bf16[]{:T(256)} %bitcast.154, bf16[]{:T(256)} %bitcast.155, bf16[]{:T(256)} %bitcast.156, bf16[]{:T(256)} %bitcast.157, ...), kind=kOutput, calls=%fused_computation.2.clone.1 | convolution fusion | flops 4423036928 | bytes 35078160 | tf_op jit(solution)/shard_map/while/body/eval_jaxpr/dot_general | solution.py:116
  97.7 23.9 %select_add_fusion.2 = f32[1038,4096]{1,0:T(8,128)} fusion(f32[1038,4096]{1,0:T(8,128)} %get-tuple-element.364, pred[]{:T(512)S(6)} %compare.38, s32[512]{0:T(512)S(1)} %get-tuple-element.320, bf16[]{:T(256)} %bitcast.153, bf16[]{:T(256)} %bitcast.154, bf16[]{:T(256)} %bitcast.155, bf16[]{:T(256)} %bitcast.156, bf16[]{:T(256)} %bitcast.157, ...), kind=kOutput, calls=%fused_computation.2.clone.1 | convolution fusion | flops 4423036928 | bytes 35078160 | tf_op jit(solution)/shard_map/while/body/eval_jaxpr/dot_general | solution.py:116
  125.3 23.9 %select_add_fusion.2 = f32[1038,4096]{1,0:T(8,128)} fusion(f32[1038,4096]{1,0:T(8,128)} %get-tuple-element.364, pred[]{:T(512)S(6)} %compare.38, s32[512]{0:T(512)S(1)} %get-tuple-element.320, bf16[]{:T(256)} %bitcast.153, bf16[]{:T(256)} %bitcast.154, bf16[]{:T(256)} %bitcast.155, bf16[]{:T(256)} %bitcast.156, bf16[]{:T(256)} %bitcast.157, ...), kind=kOutput, calls=%fused_computation.2.clone.1 | convolution fusion | flops 4423036928 | bytes 35078160 | tf_op jit(solution)/shard_map/while/body/eval_jaxpr/dot_general | solution.py:116
  152.8 23.9 %select_add_fusion.2 = f32[1038,4096]{1,0:T(8,128)} fusion(f32[1038,4096]{1,0:T(8,128)} %get-tuple-element.364, pred[]{:T(512)S(6)} %compare.38, s32[512]{0:T(512)S(1)} %get-tuple-element.320, bf16[]{:T(256)} %bitcast.153, bf16[]{:T(256)} %bitcast.154, bf16[]{:T(256)} %bitcast.155, bf16[]{:T(256)} %bitcast.156, bf16[]{:T(256)} %bitcast.157, ...), kind=kOutput, calls=%fused_computation.2.clone.1 | convolution fusion | flops 4423036928 | bytes 35078160 | tf_op jit(solution)/shard_map/while/body/eval_jaxpr/dot_general | solution.py:116
  180.4 23.9 %select_add_fusion.2 = f32[1038,4096]{1,0:T(8,128)} fusion(f32[1038,4096]{1,0:T(8,128)} %get-tuple-element.364, pred[]{:T(512)S(6)} %compare.38, s32[512]{0:T(512)S(1)} %get-tuple-element.320, bf16[]{:T(256)} %bitcast.153, bf16[]{:T(256)} %bitcast.154, bf16[]{:T(256)} %bitcast.155, bf16[]{:T(256)} %bitcast.156, bf16[]{:T(256)} %bitcast.157, ...), kind=kOutput, calls=%fused_computation.2.clone.1 | convolution fusion | flops 4423036928 | bytes 35078160 | tf_op jit(solution)/shard_map/while/body/eval_jaxpr/dot_general | solution.py:116
  207.9 23.9 %select_add_fusion.2 = f32[1038,4096]{1,0:T(8,128)} fusion(f32[1038,4096]{1,0:T(8,128)} %get-tuple-element.364, pred[]{:T(512)S(6)} %compare.38, s32[512]{0:T(512)S(1)} %get-tuple-element.320, bf16[]{:T(256)} %bitcast.153, bf16[]{:T(256)} %bitcast.154, bf16[]{:T(256)} %bitcast.155, bf16[]{:T(256)} %bitcast.156, bf16[]{:T(256)} %bitcast.157, ...), kind=kOutput, calls=%fused_computation.2.clone.1 | convolution fusion | flops 4423036928 | bytes 35078160 | tf_op jit(solution)/shard_map/while/body/eval_jaxpr/dot_general | solution.py:116
  235.4 23.9 %select_add_fusion.2 = f32[1038,4096]{1,0:T(8,128)} fusion(f32[1038,4096]{1,0:T(8,128)} %get-tuple-element.364, pred[]{:T(512)S(6)} %compare.38, s32[512]{0:T(512)S(1)} %get-tuple-element.320, bf16[]{:T(256)} %bitcast.153, bf16[]{:T(256)} %bitcast.154, bf16[]{:T(256)} %bitcast.155, bf16[]{:T(256)} %bitcast.156, bf16[]{:T(256)} %bitcast.157, ...), kind=kOutput, calls=%fused_computation.2.clone.1 | convolution fusion | flops 4423036928 | bytes 35078160 | tf_op jit(solution)/shard_map/while/body/eval_jaxpr/dot_general | solution.py:116
  259.4 13.3 %reshape.268 = f32[2,519,4096]{2,1,0:T(8,128)} reshape(f32[1038,4096]{1,0:T(8,128)} %get-tuple-element.158) | data formatting | bytes 34013184 | tf_op jit(solution)/shard_map/reshape | solution.py:148
  274.1 11.5 %slice.407 = f32[2,512,4096]{2,1,0:T(8,128)} slice(f32[2,519,4096]{2,1,0:T(8,128)} %reshape.268), slice={[0:2], [0:512], [0:4096]} | slice | bytes 33554432 | tf_op jit(solution)/shard_map/slice | solution.py:150
  288.4 10.1 slice_bitcast_fusion
  298.5 5.2 copy.103
  303.7 9.5 fusion.153
  313.2 9.7 fusion.157
  324.8 9.5 fusion.151
  334.3 18.7 %subtract_bitcast_fusion.1 = (f32[512,32,128]{2,1,0:T(8,128)}, f32[512,32,128]{2,1,0:T(8,128)}) fusion(f32[32,128]{1,0:T(8,128)S(1)} %get-tuple-element.247, f32[32,128]{1,0:T(8,128)S(1)} %get-tuple-element.248, f32[32,512,128]{2,0,1:T(8,128)} %fusion.151, f32[32,512,128]{2,0,1:T(8,128)} %fusion.157, f32[32,512,128]{2,0,1:T(8,128)} %fusion.153, ...), kind=kOutput, calls=%fused_computation.132 | convolution fusion | flops 822097920 | bytes 50364416 | tf_op jit(solution)/shard_map/rab,ak->rkb/dot_general | solution.py:53
  353.0 18.7 %fusion.82 = f32[128,512,32]{1,0,2:T(8,128)S(1)} fusion(f32[512,32,128]{2,1,0:T(8,128)} %get-tuple-element.234), kind=kOutput, calls=%fused_computation.149 | convolution fusion | flops 3221454848 | bytes 16777216 | tf_op jit(solution)/shard_map/rkb,bq->rqk/dot_general | solution.py:66
  371.8 13.6 %fusion.84 = f32[128,512,32]{1,0,2:T(8,128)} fusion(f32[512,32,128]{2,1,0:T(8,128)S(1)} %copy-done.4), kind=kOutput, calls=%fused_computation.151 | convolution fusion | flops 3221454848 | bytes 16777216 | tf_op jit(solution)/shard_map/rkb,bq->rqk/dot_general | solution.py:63
  385.4 13.9 %add_bitcast_fusion = f32[512,128,32]{0,1,2:T(8,128)} fusion(f32[128,512,32]{1,0,2:T(8,128)S(1)} %fusion.82, f32[512,32,128]{2,1,0:T(8,128)S(1)} %bitcast.170), kind=kOutput, calls=%fused_computation.129 | convolution fusion | flops 3223552000 | bytes 25165824 | tf_op jit(solution)/shard_map/rkb,bq->rqk/dot_general | solution.py:66
  399.2 8.2 copy.79
  407.5 18.9 %subtract_bitcast_fusion = f32[512,128,32]{0,1,2:T(8,128)} fusion(f32[128,512,32]{1,0,2:T(8,128)} %fusion.84, f32[512,32,128]{2,1,0:T(8,128)S(1)} %bitcast.170), kind=kOutput, calls=%fused_computation.130 | convolution fusion | flops 3223552000 | bytes 25165824 | tf_op jit(solution)/shard_map/rkb,bq->rqk/dot_general | solution.py:63
  426.4 8.2 copy.76
  434.7 5.1 fusion.100
  457.1 4.7 fusion.107
  468.1 3.4 collective-permute-start.6
  477.0 101.7 %collective-permute-done.2 = f32[2,512,1,512]{3,1,0,2:T(8,128)} collective-permute-done((f32[2,512,1,512]{3,1,0,2:T(8,128)}, f32[2,512,1,512]{3,1,0,2:T(8,128)}, u32[]{:S(2)}, u32[]{:S(2)}) %collective-permute-start.2) | collective-permute-done | bytes 2097184 | tf_op jit(solution)/shard_map/ppermute | solution.py:160
  588.0 33.8 %collective-permute-done.3 = f32[2,512,1,512]{3,1,0,2:T(8,128)} collective-permute-done((f32[2,512,1,512]{3,1,0,2:T(8,128)}, f32[2,512,1,512]{3,1,0,2:T(8,128)}, u32[]{:S(2)}, u32[]{:S(2)}) %collective-permute-start.3) | collective-permute-done | bytes 2097184 | tf_op jit(solution)/shard_map/ppermute | solution.py:160
  625.0 3.2 bitcast_dynamic-update-slice_fusion.3
  628.1 100.4 %collective-permute-done.5 = f32[2,512,1,512]{3,1,0,2:T(8,128)} collective-permute-done((f32[2,512,1,512]{3,1,0,2:T(8,128)}, f32[2,512,1,512]{3,1,0,2:T(8,128)}, u32[]{:S(2)}, u32[]{:S(2)}) %collective-permute-start.5) | collective-permute-done | bytes 2097184 | tf_op jit(solution)/shard_map/ppermute | solution.py:160
  736.3 13.9 %gather_fusion = f32[8,2,512,512]{3,2,1,0:T(8,128)} fusion(f32[8,2,512,512]{3,2,1,0:T(8,128)} %bitcast.37, s32[1024]{0:T(1024)S(1)} %pad_clamp_fusion), kind=kCustom, calls=%fused_computation | custom fusion | bytes 33554464 | tf_op jit(solution)/shard_map/gather | solution.py:163
  750.2 6.9 fusion.254
  757.1 13.2 %fusion.74 = f32[32,128,512]{2,0,1:T(8,128)} fusion(f32[32,128,512]{2,1,0:T(8,128)S(1)} %bitcast.175), kind=kOutput, calls=%fused_computation.141 | convolution fusion | flops 805320704 | bytes 16777216 | tf_op jit(solution)/shard_map/abc,ak->kbc/dot_general | solution.py:81
  770.3 13.2 %fusion.76 = f32[32,128,512]{2,0,1:T(8,128)} fusion(f32[32,128,512]{2,1,0:T(8,128)S(1)} %bitcast.176), kind=kOutput, calls=%fused_computation.143 | convolution fusion | flops 805320704 | bytes 16777216 | tf_op jit(solution)/shard_map/abc,ak->kbc/dot_general | solution.py:78
  783.6 13.2 %fusion.80 = f32[32,128,512]{2,0,1:T(8,128)} fusion(f32[32,128,512]{2,1,0:T(8,128)S(1)} %bitcast.177), kind=kOutput, calls=%fused_computation.147 | convolution fusion | flops 805320704 | bytes 16777216 | tf_op jit(solution)/shard_map/abc,ak->kbc/dot_general | solution.py:78
  796.7 24.5 %multiply_subtract_fusion = (f32[32,128,512]{2,0,1:T(8,128)}, f32[32,128,512]{2,0,1:T(8,128)}) fusion(f32[32,128]{0,1:T(8,128)S(1)} %copy.93, f32[32,128]{0,1:T(8,128)S(1)} %copy.90, f32[32,128,512]{2,0,1:T(8,128)} %fusion.74, f32[32,128,512]{2,0,1:T(8,128)} %fusion.80, f32[32,128,512]{2,0,1:T(8,128)} %fusion.76, f32[32,128,512]{2,1,0:T(8,128)} %bitcast.178), kind=kOutput, calls=%fused_computation.128 | convolution fusion | flops 822097920 | bytes 50364416 | tf_op jit(solution)/shard_map/abc,ak->kbc/dot_general | solution.py:81
  821.2 17.0 %fusion.68 = f32[128,32,512]{2,0,1:T(8,128)S(1)} fusion(f32[32,128,512]{2,0,1:T(8,128)} %get-tuple-element.232), kind=kOutput, calls=%fused_computation.135 | convolution fusion | flops 3221454848 | bytes 16777216 | tf_op jit(solution)/shard_map/kbc,bq->qkc/dot_general | solution.py:88
  838.3 13.4 %fusion.66 = f32[128,32,512]{2,0,1:T(8,128)} fusion(f32[32,128,512]{2,0,1:T(8,128)S(1)} %copy-done.2), kind=kOutput, calls=%fused_computation.133 | convolution fusion | flops 3221454848 | bytes 16777216 | tf_op jit(solution)/shard_map/kbc,bq->qkc/dot_general | solution.py:91
  851.6 13.6 %fusion.94 = f32[128,32,512]{2,0,1:T(8,128)} fusion(f32[128,32,512]{2,0,1:T(8,128)S(1)} %fusion.68, f32[32,128,512]{2,0,1:T(8,128)S(1)} %bitcast.168), kind=kOutput, calls=%fused_computation.157 | convolution fusion | flops 3223552000 | bytes 25165824 | tf_op jit(solution)/shard_map/kbc,bq->qkc/dot_general | solution.py:88
  865.3 8.2 copy.96
  873.5 15.6 %fusion.97 = f32[128,32,512]{2,0,1:T(8,128)} fusion(f32[128,32,512]{2,0,1:T(8,128)} %fusion.66, f32[32,128,512]{2,0,1:T(8,128)S(1)} %bitcast.168), kind=kOutput, calls=%fused_computation.158 | convolution fusion | flops 3223552000 | bytes 25165824 | tf_op jit(solution)/shard_map/kbc,bq->qkc/dot_general | solution.py:91
  889.2 8.2 copy.99
  897.4 36.1 %fusion.65 = f32[4096,512]{1,0:T(8,128)} fusion(f32[128,32,512]{2,1,0:T(8,128)S(1)} %copy.99, f32[128,32,512]{2,1,0:T(8,128)S(1)} %copy.96, f32[512]{0:T(512)S(1)} %fusion.202, f32[4096]{0:T(1024)S(1)} %fusion.142, f32[]{:T(128)} %bitcast), kind=kLoop, calls=%fused_computation.125 | loop fusion | flops 12582912 | bytes 25184260 | tf_op jit(solution)/shard_map/sub | solution.py:179
  933.5 168.5 %reduce-scatter.2.cloned.1.call-done = f32[1024,512]{1,0:T(8,128)} async-done(((f32[4096,512]{1,0:T(8,128)}), f32[1024,512]{1,0:T(8,128)}) %reduce-scatter.2.cloned.1.call-update) | async-done | bytes 2097168 | tf_op jit(solution)/shard_map/reduce_scatter | solution.py:180
  (141 shorter events, 93.0 us)
Async XLA Ops:
  27.7 14.7 %all-to-all-start = ((f32[3,32,128]{2,0,1:T(4,128)}), f32[3,32,128]{2,0,1:T(4,128)S(1)}, u32[]{:S(2)}, u32[]{:S(2)}) async-start(f32[3,32,128]{2,0,1:T(4,128)} %copy.73), calls=%async_computation | async-start | bytes 131072 | tf_op jit(solution)/shard_map/all_to_all | solution.py:140
  35.1 1067.0 %reduce-scatter.2.cloned.1.call-start = ((), (), s32[]{:S(2)}) async-start(), calls=%async_computation.2 | async-start | bytes 10485760 | tf_op jit(solution)/shard_map/reduce_scatter | solution.py:180
  273.6 12.0 %collective-permute-start = (f32[2,7,4096]{2,1,0:T(8,128)S(1)}, f32[2,7,4096]{2,1,0:T(8,128)S(1)}, u32[]{:S(2)}, u32[]{:S(2)}) collective-permute-start(f32[2,7,4096]{2,1,0:T(8,128)S(1)} %slice.409), channel_id=1, source_target_pairs={{0,1},{1,2},{2,3},{3,4},{4,5},{5,6},{6,7},{7,0},{8,9},{9,10},{10,1... | collective-permute-start | bytes 688136 | tf_op jit(solution)/shard_map/ppermute | solution.py:25
  324.8 9.5 copy-start.3
  353.0 18.8 %copy-start.4 = (f32[512,32,128]{2,1,0:T(8,128)S(1)}, f32[512,32,128]{2,1,0:T(8,128)}, u32[]{:S(2)}) copy-start(f32[512,32,128]{2,1,0:T(8,128)} %get-tuple-element.234) | copy-start | bytes 25165828
  353.0 32.3 %slice-start.2 = ((s8[8388608]{0:T(1024)(128)(4,1)}), s8[4194304]{0:T(1024)(128)(4,1)S(1)}, s32[]{:S(2)}) async-start(s8[8388608]{0:T(1024)(128)(4,1)} %bitcast.169), calls=%async_computation.5 | async-start | bytes 8388608
  371.8 13.6 %slice-start.3 = ((s8[8388608]{0:T(1024)(128)(4,1)}), s8[4194304]{0:T(1024)(128)(4,1)S(1)}, s32[]{:S(2)}) async-start(s8[8388608]{0:T(1024)(128)(4,1)} %bitcast.169), calls=%async_computation.6 | async-start | bytes 8388608
  407.5 27.2 %copy-start = (f32[512,128,32]{0,2,1:T(8,128)}, f32[512,128,32]{0,2,1:T(8,128)S(1)}, u32[]{:S(2)}) copy-start(f32[512,128,32]{0,2,1:T(8,128)S(1)} %copy.79) | copy-start | bytes 25165828
  434.7 6.4 copy-start.1
  444.0 24.1 %collective-permute-start.1 = (f32[2,512,1,512]{3,1,0,2:T(8,128)}, f32[2,512,1,512]{3,1,0,2:T(8,128)}, u32[]{:S(2)}, u32[]{:S(2)}) collective-permute-start(f32[2,512,1,512]{3,1,0,2:T(8,128)} %bitcast.185), channel_id=1, source_target_pairs={{0,1},{1,0},{2,3},{3,2},{4,5},{5,4},{6,7},{7,6},{8,9},{9,8},{10,11... | collective-permute-start | bytes 6291464 | tf_op jit(solution)/shard_map/ppermute | solution.py:160
  447.3 131.5 %collective-permute-start.2 = (f32[2,512,1,512]{3,1,0,2:T(8,128)}, f32[2,512,1,512]{3,1,0,2:T(8,128)}, u32[]{:S(2)}, u32[]{:S(2)}) collective-permute-start(f32[2,512,1,512]{3,1,0,2:T(8,128)} %bitcast.183), channel_id=1, source_target_pairs={{0,2},{1,3},{2,0},{3,1},{4,6},{5,7},{6,4},{7,5},{8,10},{9,11},{10,... | collective-permute-start | bytes 6291464 | tf_op jit(solution)/shard_map/ppermute | solution.py:160
  450.7 171.2 %collective-permute-start.3 = (f32[2,512,1,512]{3,1,0,2:T(8,128)}, f32[2,512,1,512]{3,1,0,2:T(8,128)}, u32[]{:S(2)}, u32[]{:S(2)}) collective-permute-start(f32[2,512,1,512]{3,1,0,2:T(8,128)} %bitcast.182), channel_id=1, source_target_pairs={{0,3},{1,2},{2,1},{3,0},{4,7},{5,6},{6,5},{7,4},{8,11},{9,10},{10,... | collective-permute-start | bytes 6291464 | tf_op jit(solution)/shard_map/ppermute | solution.py:160
  454.6 170.4 %collective-permute-start.4 = (f32[2,512,1,512]{3,1,0,2:T(8,128)}, f32[2,512,1,512]{3,1,0,2:T(8,128)}, u32[]{:S(2)}, u32[]{:S(2)}) collective-permute-start(f32[2,512,1,512]{3,1,0,2:T(8,128)} %bitcast.181), channel_id=1, source_target_pairs={{0,4},{1,5},{2,6},{3,7},{4,0},{5,1},{6,2},{7,3},{8,12},{9,13},{10,... | collective-permute-start | bytes 6291464 | tf_op jit(solution)/shard_map/ppermute | solution.py:160
  464.7 263.9 %collective-permute-start.5 = (f32[2,512,1,512]{3,1,0,2:T(8,128)}, f32[2,512,1,512]{3,1,0,2:T(8,128)}, u32[]{:S(2)}, u32[]{:S(2)}) collective-permute-start(f32[2,512,1,512]{3,1,0,2:T(8,128)} %bitcast.184), channel_id=1, source_target_pairs={{0,5},{1,4},{2,7},{3,6},{4,1},{5,0},{6,3},{7,2},{8,13},{9,12},{10,... | collective-permute-start | bytes 6291464 | tf_op jit(solution)/shard_map/ppermute | solution.py:160
  468.1 263.5 %collective-permute-start.6 = (f32[2,512,1,512]{3,1,0,2:T(8,128)}, f32[2,512,1,512]{3,1,0,2:T(8,128)}, u32[]{:S(2)}, u32[]{:S(2)}) collective-permute-start(f32[2,512,1,512]{3,1,0,2:T(8,128)} %bitcast.186), channel_id=1, source_target_pairs={{0,6},{1,7},{2,4},{3,5},{4,2},{5,3},{6,0},{7,1},{8,14},{9,15},{10,... | collective-permute-start | bytes 6291464 | tf_op jit(solution)/shard_map/ppermute | solution.py:160
  578.8 156.0 %collective-permute-start.7 = (f32[2,512,1,512]{3,1,0,2:T(8,128)}, f32[2,512,1,512]{3,1,0,2:T(8,128)S(1)}, u32[]{:S(2)}, u32[]{:S(2)}) collective-permute-start(f32[2,512,1,512]{3,1,0,2:T(8,128)} %bitcast.187), channel_id=1, source_target_pairs={{0,7},{1,6},{2,5},{3,4},{4,3},{5,2},{6,1},{7,0},{8,15},{9,14},{10,... | collective-permute-start | bytes 6291464 | tf_op jit(solution)/shard_map/ppermute | solution.py:160
  757.1 26.4 %copy-start.5 = (f32[1,8,512,1,512]{4,2,0,1,3:T(8,128)}, f32[1,8,512,1,512]{4,2,0,1,3:T(8,128)S(1)}, u32[]{:S(2)}) copy-start(f32[1,8,512,1,512]{4,2,0,1,3:T(8,128)S(1)} %get-tuple-element.236) | copy-start | bytes 25165828
  821.2 17.0 %copy-start.2 = (f32[32,128,512]{2,0,1:T(8,128)S(1)}, f32[32,128,512]{2,0,1:T(8,128)}, u32[]{:S(2)}) copy-start(f32[32,128,512]{2,0,1:T(8,128)} %get-tuple-element.232) | copy-start | bytes 25165828
  821.2 30.4 %slice-start = ((s8[8388608]{0:T(1024)(128)(4,1)}), s8[4194304]{0:T(1024)(128)(4,1)S(1)}, s32[]{:S(2)}) async-start(s8[8388608]{0:T(1024)(128)(4,1)} %bitcast.167), calls=%async_computation.3 | async-start | bytes 8388608
  838.3 13.4 %slice-start.1 = ((s8[8388608]{0:T(1024)(128)(4,1)}), s8[4194304]{0:T(1024)(128)(4,1)S(1)}, s32[]{:S(2)}) async-start(s8[8388608]{0:T(1024)(128)(4,1)} %bitcast.167), calls=%async_computation.4 | async-start | bytes 8388608
Sparse Core Ops, SparseCore 0:
  933.7 168.3 reduce-scatter.1
